TPU v7x, 32 devices: a 4x4x1 block of a 4x4x8 slice. The times are simulated.
32 devices in a mesh: dp: 1 (over z), sp: 32 (over x, y, core).
Axes of the slice: x: 4, y: 4, z: 1, core: 2. Of those that a mesh axis runs over, the one named last changes fastest.
The devices are a block of a 4x4x8 slice.
Arguments:
- q: bfloat16 [32, 8, 256], P('dp')
- k: bfloat16 [32, 8192, 8, 256], P('dp', 'sp')
- v: bfloat16 [32, 8192, 8, 256], P('dp', 'sp')
Outputs:
- q: bfloat16 [32, 8, 256], P('dp')
All inputs are finite; a program needn't handle non-finite values.
Results may differ from a plain program's by a relative error of at most 0.012.
Values are sent between devices in bfloat16 or wider.
A program may use at most 768 MiB of HBM per device.

v0:
```python
import jax
import jax.numpy as jnp
from jax import lax
from jax.sharding import PartitionSpec as P


def einsum(form, a, b):
    return jnp.einsum(form, a.astype(jnp.float32), b.astype(jnp.float32))


def part_of(q, k, v):
    grouped = q.reshape(q.shape[0], k.shape[2], -1, q.shape[2])
    scores = einsum("bgsd,bugd->bgsu", grouped, k) * q.shape[2] ** -0.5
    high = jnp.max(scores, -1, keepdims=True)
    weights = jnp.exp(scores - high)
    seen = einsum("bgsu,bugd->bgsd", weights.astype(jnp.bfloat16), v)
    return jnp.concatenate([seen, jnp.sum(weights, -1, keepdims=True), high], -1)


def together(parts):
    seen, total, high = parts[..., :-2], parts[..., -2:-1], parts[..., -1:]
    scale = jnp.exp(high - jnp.max(high, 0))
    return (jnp.sum(seen * scale, 0) / jnp.sum(total * scale, 0)).astype(jnp.bfloat16)


def solution(mesh):
    def step(q, k, v):
        return together(lax.all_gather(part_of(q, k, v), "sp")).reshape(q.shape)

    return jax.shard_map(
        step,
        mesh=mesh,
        in_specs=(P("dp", None, None), P("dp", "sp", None, None), P("dp", "sp", None, None)),
        out_specs=P("dp", None, None),
        check_vma=False,
    )
```

profile of v0, /device:TPU:97, one launch (start us, length us, event | category | flops | bytes accessed | tf_op | source)
XLA Modules:
  0.0 137.5 jit_solution(4843364689182857839)
XLA Ops:
  6.5 0.0 all-gather.3.cloned.1.call-start
  6.6 18.1 %fusion.2 = f32[32,8,1,256]{3,2,1,0:T(1,128)S(1)} fusion(bf16[32,256,8,256]{3,2,1,0:T(8,128)(2,1)} %param.4, bf16[32,8,256,1]{2,1,0,3:T(8,128)(2,1)} %bitcast.27), kind=kOutput, calls=%fused_computation.2 | convolution fusion | flops 33554432 | bytes 33947648 | tf_op jit(solution)/shard_map/bgsd,bugd->bgsu/dot_general | solution.py:8
  24.6 0.1 fusion.10
  24.8 0.2 fusion.11
  24.9 0.3 copy.23
  25.2 0.3 copy.22
  25.5 19.1 %fusion = f32[32,8,1,256]{3,2,1,0:T(1,128)S(1)} fusion(bf16[32,256,8,256]{3,2,1,0:T(8,128)(2,1)} %param.5, bf16[32,8,256,1]{2,1,0,3:T(8,128)(2,1)S(1)} %get-tuple-element.7), kind=kOutput, calls=%fused_computation | convolution fusion | flops 33554432 | bytes 33947648 | tf_op jit(solution)/shard_map/bgsu,bugd->bgsd/dot_general | solution.py:8
  44.6 0.9 pad_maximum_fusion
  45.5 0.1 all-gather.3.cloned.1.call-update
  45.5 61.8 %all-gather.3.cloned.1.call-done = f32[1024,8,1,258]{3,1,2,0:T(8,128)} async-done(((f32[32,8,1,258]{3,1,2,0:T(8,128)}), f32[1024,8,1,258]{3,1,2,0:T(8,128)}) %all-gather.3.cloned.1.call-update) | async-done | bytes 8454160 | tf_op jit(solution)/shard_map/all_gather | solution.py:28
  107.3 3.5 %slice_reduce_fusion = f32[32,8]{1,0:T(8,128)S(1)} fusion(f32[32,32,8,1,258]{4,2,1,0,3:T(8,128)} %bitcast.22), kind=kLoop, calls=%fused_computation.9 | loop fusion | flops 7936 | bytes 33792 | tf_op jit(solution)/shard_map/reduce_max | solution.py:22
  110.8 7.1 %fusion.5 = (f32[32,8]{1,0:T(8,128)S(1)}, f32[32,32,8,1,1]{4,2,1,0,3:T(8,128)}) fusion(f32[32,32,8,1,258]{4,2,1,0,3:T(8,128)} %bitcast.23, f32[32,8]{1,0:T(8,128)S(1)} %slice_reduce_fusion), kind=kLoop, calls=%fused_computation.7 | loop fusion | flops 24320 | bytes 100352 | tf_op jit(solution)/shard_map/reduce_sum | solution.py:23
  118.0 7.7 %copy.36 = f32[32,32,8,1,1]{2,1,0,3,4:T(8,128)S(1)} copy(f32[32,32,8,1,1]{4,2,1,0,3:T(8,128)} %get-tuple-element.6) | data formatting | bytes 65536 | tf_op jit(solution)/shard_map/mul | solution.py:23
  125.6 4.2 %fusion.4 = f32[32,8,256]{2,1,0:T(8,128)S(1)} fusion(f32[32,32,8,1,258]{4,2,1,0,3:T(8,128)} %bitcast.24, f32[32,32,8]{2,1,0:T(8,128)S(1)} %bitcast.25), kind=kLoop, calls=%fused_computation.5 | loop fusion | flops 4128768 | bytes 8683520 | tf_op jit(solution)/shard_map/reduce_sum | solution.py:23
  129.9 0.8 divide_convert_fusion
  (1 shorter events, 0.0 us)
Async XLA Ops:
  6.5 100.8 %all-gather.3.cloned.1.call-start = ((), (), s32[]{:S(2)}) async-start(), calls=%async_computation | async-start | bytes 12976128 | tf_op jit(solution)/shard_map/all_gather | solution.py:28
Sparse Core Ops, SparseCore 0:
  45.7 61.5 all-gather.2
where the time goes:
time: 138 us; the launch traced here: 137 us
  waiting for transfers between devices  61.8 us (45%)
  matrix products  37.2 us (27%)
  other arithmetic  16.8 us (12%)
  between operations  13.5 us (10%)
  local copies, waits for them, and re-layouts  8.21 us (6%)
    all_gather x1, waiting for transfers between devices, step(): return together(lax.all_gather(part_of(q, k, v), 'sp')).reshape(q.shape)  61.8 us
    dot_general x2, matrix products, einsum(): return jnp.einsum(form, a.astype(jnp.float32), b.astype(jnp.float32))  37.2 us
    mul x1, local copies, waits for them, and re-layouts, together(): seen * scale  7.67 us
    reduce_sum x1, other arithmetic, together(): jnp.sum(total * scale, 0)  7.13 us
    reduce_sum x1, other arithmetic, together(): jnp.sum(seen * scale, 0) / jnp.sum(total * scale, 0)  4.22 us
    reduce_max x1, other arithmetic, together(): scale = jnp.exp(high - jnp.max(high, 0))  3.52 us
  transfers between devices with their start and end apart: 1, of which 1 were waited for; matrix products, arithmetic and copies ran while one was open for 0% of the time, Pallas kernels for 0%

commit v1 on v0

v1 whole, which is shorter than its diff:
```python
import functools
import math

import jax
import jax.numpy as jnp
from jax import lax
from jax.experimental import pallas as pl
from jax.experimental.pallas import tpu as pltpu
from jax.sharding import PartitionSpec as P

MESH = pl.DeviceIdType.MESH
GROUP = 2
SLOTS = 8
LAG1 = 3
LAG2 = 6


def kernel(inner, outer, heads, q_ref, k_hbm, v_hbm, o_ref, kbuf, vbuf, parts1, stats1, parts2, stats2, ksem, vsem, sent1, sent2, got1, got2, statsent1, statsent2, statgot1, statgot2):
    steps, _, rows, head = parts1.shape
    tokens = k_hbm.shape[1]
    me, group = lax.axis_index("sp"), lax.axis_index("dp")
    row, col = lax.div(me, inner), lax.rem(me, inner)
    peers1 = [row * inner + lax.rem(col + j, inner) for j in range(1, inner)]
    peers2 = [lax.rem(row + j, outer) * inner + col for j in range(1, outer)]

    def fetch(hbm, buf, sem, i):
        slot = lax.rem(i, SLOTS)
        return pltpu.make_async_copy(hbm.at[pl.ds(i * GROUP, GROUP)], buf.at[slot], sem.at[slot])

    def prefetch(i, _):
        fetch(k_hbm, kbuf, ksem, i).start()
        fetch(v_hbm, vbuf, vsem, i).start()
        return 0

    lax.fori_loop(0, min(SLOTS, steps), prefetch, 0)

    barrier = pltpu.get_barrier_semaphore()
    for peer in peers1 + peers2:
        pl.semaphore_signal(barrier, inc=1, device_id=(group, peer), device_id_type=MESH)

    own = lax.rem(lax.broadcasted_iota(jnp.int32, (heads, tokens), 1), heads) == lax.broadcasted_iota(jnp.int32, (heads, tokens), 0)
    eye = lax.broadcasted_iota(jnp.int32, (rows, 128), 1) == lax.broadcasted_iota(jnp.int32, (rows, 128), 0)

    def across(column):
        return jnp.sum(jnp.where(eye, column, 0.0), 0, keepdims=True)

    def down(line):
        return jnp.sum(jnp.where(eye, line, 0.0), 1, keepdims=True)

    def send(parts, stats, i, mine, peers, sent, got, statsent, statgot):
        for ref, out, into in ((parts, sent, got), (stats, statsent, statgot)):
            for peer in peers:
                pltpu.make_async_remote_copy(
                    src_ref=ref.at[i, mine], dst_ref=ref.at[i, mine], send_sem=out, recv_sem=into.at[i], device_id=(group, peer), device_id_type=MESH
                ).start()

    def arrived(ref, i, count, sem):
        part = ref.at[i, pl.ds(0, count)]
        pltpu.make_async_copy(part, part, sem.at[i]).wait()

    def attend(i):
        slot = lax.rem(i, SLOTS)
        fetch(k_hbm, kbuf, ksem, i).wait()
        scores = []
        for g in range(GROUP):
            scores.append(lax.dot_general(q_ref[i * GROUP + g], kbuf[slot, g], (((1,), (1,)), ((), ())), preferred_element_type=jnp.float32))
        highs, totals, weights = [], [], []
        for g in range(GROUP):
            s = jnp.where(own, scores[g] * head**-0.5, -jnp.inf)
            high = jnp.max(s, 1, keepdims=True)
            w = jnp.exp(s - high)
            highs.append(high)
            totals.append(jnp.sum(w, 1, keepdims=True))
            weights.append(w.astype(jnp.bfloat16))
        fetch(v_hbm, vbuf, vsem, i).wait()
        seen = [jnp.dot(weights[g], vbuf[slot, g], preferred_element_type=jnp.float32) for g in range(GROUP)]
        parts1[i, col] = jnp.concatenate(seen, 0).astype(jnp.bfloat16)
        stats1[i, col] = jnp.concatenate([across(jnp.concatenate(highs, 0)), across(jnp.concatenate(totals, 0))], 0)

    def merge(parts, stats, i, count):
        high = stats[i, :, 0, :]
        top = jnp.max(high, 0, keepdims=True)
        scale = jnp.exp(high - top)
        total = jnp.sum(stats[i, :, 1, :] * scale, 0, keepdims=True)
        seen = sum(down(scale[s : s + 1]) * parts[i, s].astype(jnp.float32) for s in range(count))
        return seen, total, top

    def first(i):
        arrived(parts1, i, inner - 1, got1)
        arrived(stats1, i, inner - 1, statgot1)
        seen, total, top = merge(parts1, stats1, i, inner)
        parts2[i, row] = seen.astype(jnp.bfloat16)
        stats2[i, row] = jnp.concatenate([top, total], 0)
        send(parts2, stats2, i, row, peers2, sent2, got2, statsent2, statgot2)

    def second(i):
        arrived(parts2, i, outer - 1, got2)
        arrived(stats2, i, outer - 1, statgot2)
        seen, total, _ = merge(parts2, stats2, i, outer)
        o_ref[pl.ds(i * rows, rows), :] = (seen / down(total)).astype(o_ref.dtype)

    def step(i, _):
        attend(i)

        @pl.when(i == 0)
        def _():
            pl.semaphore_wait(barrier, inner + outer - 2)

        send(parts1, stats1, i, col, peers1, sent1, got1, statsent1, statgot1)

        @pl.when(i + SLOTS < steps)
        def _():
            prefetch(i + SLOTS, 0)

        @pl.when(i >= LAG1)
        def _():
            first(i - LAG1)

        @pl.when(i >= LAG2)
        def _():
            second(i - LAG2)

        return 0

    lax.fori_loop(0, steps, step, 0)

    def drain(i, _):
        @pl.when(i - LAG1 < steps)
        def _():
            first(i - LAG1)

        second(i - LAG2)
        return 0

    lax.fori_loop(steps, steps + LAG2, drain, 0)

    for ref, count, sem in ((parts1, inner - 1, sent1), (parts2, outer - 1, sent2), (stats1, inner - 1, statsent1), (stats2, outer - 1, statsent2)):
        part = ref.at[:, pl.ds(0, count)]
        pltpu.make_async_copy(part, part, sem).wait()


def solution(mesh):
    n = mesh.shape["sp"]
    outer = math.isqrt(n // 2)
    inner = n // outer

    def step(q, k, v):
        batch, tokens, heads, head = k.shape
        steps, rows = batch // GROUP, GROUP * heads
        k, v = (a.reshape(batch, tokens * heads, head) for a in (k, v))
        out = pl.pallas_call(
            functools.partial(kernel, inner, outer, heads),
            out_shape=jax.ShapeDtypeStruct((batch * heads, head), q.dtype),
            in_specs=[pl.BlockSpec(memory_space=pltpu.VMEM), pl.BlockSpec(memory_space=pl.ANY), pl.BlockSpec(memory_space=pl.ANY)],
            out_specs=pl.BlockSpec(memory_space=pltpu.VMEM),
            scratch_shapes=[
                pltpu.VMEM((SLOTS, GROUP, tokens * heads, head), k.dtype),
                pltpu.VMEM((SLOTS, GROUP, tokens * heads, head), v.dtype),
                pltpu.VMEM((steps, inner, rows, head), jnp.bfloat16),
                pltpu.VMEM((steps, inner, 2, 128), jnp.float32),
                pltpu.VMEM((steps, outer, rows, head), jnp.bfloat16),
                pltpu.VMEM((steps, outer, 2, 128), jnp.float32),
                pltpu.SemaphoreType.DMA((SLOTS,)),
                pltpu.SemaphoreType.DMA((SLOTS,)),
                pltpu.SemaphoreType.DMA,
                pltpu.SemaphoreType.DMA,
                pltpu.SemaphoreType.DMA((steps,)),
                pltpu.SemaphoreType.DMA((steps,)),
                pltpu.SemaphoreType.DMA,
                pltpu.SemaphoreType.DMA,
                pltpu.SemaphoreType.DMA((steps,)),
                pltpu.SemaphoreType.DMA((steps,)),
            ],
            compiler_params=pltpu.CompilerParams(collective_id=0, has_side_effects=True, vmem_limit_bytes=60 * 2**20),
        )(q, k, v)
        return out.reshape(q.shape)

    return jax.shard_map(
        step,
        mesh=mesh,
        in_specs=(P("dp", None, None), P("dp", "sp", None, None), P("dp", "sp", None, None)),
        out_specs=P("dp", None, None),
        check_vma=False,
    )
```

time: 138 us -> 43.2 us (0.31)
  waiting for transfers between devices: 61.8 us -> 0 us
  Pallas kernels: 0 us -> 41.5 us
  matrix products: 37.2 us -> 0 us
  other arithmetic: 16.8 us -> 0 us
  between operations: 13.5 us -> 0.01 us
  local copies, waits for them, and re-layouts: 8.21 us -> 1.57 us
    all_gather x1 -> x0, waiting for transfers between devices: 61.8 us -> none  [step(): return together(lax.all_gather(part_of(q, k, v), 'sp')).reshape(q.shape)]
    pallas_call x0 -> x1, Pallas kernels: none -> 41.5 us  [step(): pl.pallas_call(functools.partial(kernel, inner, outer, heads), out_shape=...]
    dot_general x2 -> x0, matrix products: 37.2 us -> none  [einsum(): return jnp.einsum(form, a.astype(jnp.float32), b.astype(jnp.float32))]
    reduce_sum x2 -> x0, other arithmetic: 11.4 us -> none  [the longest x1 7.13 us: together(): jnp.sum(total * scale, 0)]
    mul x1 -> x0, local copies, waits for them, and re-layouts: 7.67 us -> none  [together(): seen * scale]
    reduce_max x2 -> x0, other arithmetic: 3.64 us -> none  [the longest x1 3.52 us: together(): scale = jnp.exp(high - jnp.max(high, 0))]
    unnamed x0 -> x1, local copies, waits for them, and re-layouts: none -> 1.57 us
  transfers between devices with their start and end apart: 1 -> 0, of which waited for: 1 -> 0; matrix products, arithmetic and copies ran while one was open for 0% -> 0% of each run, Pallas kernels for 0% -> 0%
where the time goes in v1:
time: 43.2 us; the launch traced here: 43.1 us
  Pallas kernels  41.5 us (96%)
  local copies, waits for them, and re-layouts  1.57 us (4%)
    pallas_call x1, Pallas kernels, step(): pl.pallas_call(functools.partial(kernel, inner, outer, heads), out_shape=...  41.5 us
    unnamed x1, local copies, waits for them, and re-layouts  1.57 us

profile of v1, /device:TPU:97, one launch (start us, length us, event | category | flops | bytes accessed | tf_op | source)
XLA Modules:
  0.0 43.1 jit_solution(18321276656246804631)
XLA Ops:
  0.0 41.5 %shard_map.37 = bf16[256,256]{1,0:T(8,128)(2,1)} custom-call(bf16[32,8,256]{2,1,0:T(8,128)(2,1)} %q_ref.1, bf16[32,2048,256]{2,1,0:T(8,128)(2,1)} %bitcast.3, bf16[32,2048,256]{2,1,0:T(8,128)(2,1)} %bitcast.4), custom_call_target="tpu_custom_call" | custom-call | tf_op jit(solution)/shard_map/pallas_call | solution.py:151
  41.5 1.6 %copy.5 = bf16[32,8,256]{2,1,0:T(8,128)(2,1)} copy(bf16[32,8,256]{2,1,0:T(8,128)(2,1)} %bitcast.5) | data formatting | bytes 262144

commit v2 on v0

v2 whole, which is shorter than its diff:
```python
import jax
import jax.numpy as jnp
from jax import lax
from jax.experimental import pallas as pl
from jax.experimental.pallas import tpu as pltpu
from jax.sharding import PartitionSpec as P

MESH = pl.DeviceIdType.MESH
GROUP = 2
SLOTS = 8
GREET = 6
DIRECT = 0


def kernel(
    q_hbm, k_hbm, v_hbm, o_ref, q_ref, kbuf, vbuf, scores, mine, mine_stats, owned, owned_stats, direct, direct_stats, done,
    qsem, ksem, vsem, mine_sent, mine_stats_sent, owned_got, owned_stats_got, done_sent, done_got, direct_sent, direct_stats_sent, direct_got, direct_stats_got,
):
    batch, tokens, head = k_hbm.shape
    heads, n = q_ref.shape[1], owned.shape[0]
    steps, owners = batch // GROUP, mine.shape[0]
    last = owners // GROUP
    me, group = lax.axis_index("sp"), lax.axis_index("dp")
    my_seq = jnp.maximum(owners - 1 - me, 0)
    owner = me < owners

    def fetch(hbm, buf, sem, i):
        slot = lax.rem(i, SLOTS)
        return pltpu.make_async_copy(hbm.at[pl.ds(i * GROUP, GROUP)], buf.at[slot], sem.at[slot])

    def each(low, high, act):
        def body(i, _):
            act(i)
            return 0

        lax.fori_loop(low, high, body, 0)

    def prefetch(i):
        fetch(k_hbm, kbuf, ksem, i).start()
        fetch(v_hbm, vbuf, vsem, i).start()

    pltpu.make_async_copy(q_hbm, q_ref, qsem).start()
    each(0, min(SLOTS, steps), prefetch)

    def others(act):
        each(1, n, lambda j: act(lax.rem(me + j, n)))

    barrier = pltpu.get_barrier_semaphore()
    others(lambda peer: pl.semaphore_signal(barrier, inc=1, device_id=(group, peer), device_id_type=MESH))

    own = lax.rem(lax.broadcasted_iota(jnp.int32, (heads, tokens), 1), heads) == lax.broadcasted_iota(jnp.int32, (heads, tokens), 0)
    place = lax.broadcasted_iota(jnp.int32, (heads, 128), 1) - lax.broadcasted_iota(jnp.int32, (heads, 128), 0)
    eyes = [place == g * heads for g in range(GROUP)]

    def across(column, g=0):
        return jnp.sum(jnp.where(eyes[g], column, 0.0), 0, keepdims=True)

    def down(line, g=0):
        return jnp.sum(jnp.where(eyes[g], line, 0.0), 1, keepdims=True)

    def send(src, dst, sent, got, peer):
        pltpu.make_async_remote_copy(src_ref=src, dst_ref=dst, send_sem=sent, recv_sem=got, device_id=(group, peer), device_id_type=MESH).start()

    def wait(ref, sem):
        pltpu.make_async_copy(ref, ref, sem).wait()

    def score(i):
        slot = lax.rem(i, SLOTS)
        for g in range(GROUP):
            scores[lax.rem(i, 2), g] = lax.dot_general(q_ref[i * GROUP + g], kbuf[slot, g], (((1,), (1,)), ((), ())), preferred_element_type=jnp.float32)

    def attend(i, early):
        slot = lax.rem(i, SLOTS)
        highs, totals = [], []
        for g in range(GROUP):
            s = jnp.where(own, scores[lax.rem(i, 2), g] * head**-0.5, -jnp.inf)
            high = jnp.max(s, 1, keepdims=True)
            w = jnp.exp(s - high)
            total = jnp.sum(w, 1, keepdims=True)
            seen = jnp.dot(w.astype(jnp.bfloat16), vbuf[slot, g], preferred_element_type=jnp.float32).astype(jnp.bfloat16)
            if early:
                mine[i * GROUP + g] = seen
                mine_stats[i * GROUP + g] = jnp.concatenate([across(high), across(total)], 0)
            else:
                direct[i - last, me, g] = seen
                highs.append(across(high, g))
                totals.append(across(total, g))
        if not early:
            direct_stats[i - last, me] = jnp.concatenate([sum(highs), sum(totals)], 0)

    def to_owners(i):
        for g in range(GROUP):
            seq = i * GROUP + g
            to = owners - 1 - seq

            @pl.when(me != to)
            def _():
                send(mine.at[seq], owned.at[me], mine_sent, owned_got, to)
                send(mine_stats.at[seq], owned_stats.at[me], mine_stats_sent, owned_stats_got, to)

    def to_all(i):
        def both(peer):
            send(direct.at[i - last, me], direct.at[i - last, me], direct_sent, direct_got.at[i - last], peer)
            send(direct_stats.at[i - last, me], direct_stats.at[i - last, me], direct_stats_sent, direct_stats_got.at[i - last], peer)

        others(both)

    def merge(stats, parts):
        high = stats[:, 0, :]
        top = jnp.max(high, 0, keepdims=True)
        scale = jnp.exp(high - top)
        total = jnp.sum(stats[:, 1, :] * scale, 0, keepdims=True)
        outs = []
        for g, part in enumerate(parts):
            seen = sum(down(scale[s : s + 1], g) * part[s].astype(jnp.float32) for s in range(n))
            outs.append((seen / down(total, g)).astype(jnp.bfloat16))
        return outs

    def step(i, early, greeted=True, ahead=True):
        if ahead:
            fetch(k_hbm, kbuf, ksem, i + 1).wait()
        fetch(v_hbm, vbuf, vsem, i).wait()
        if ahead:
            score(i + 1)
        attend(i, early)
        if early and greeted:
            to_owners(i)
        if not early:
            to_all(i)
        if ahead:

            @pl.when(i + SLOTS < steps)
            def _():
                prefetch(i + SLOTS)

    wait(q_ref, qsem)
    fetch(k_hbm, kbuf, ksem, 0).wait()
    score(0)
    each(0, GREET, lambda i: step(i, True, greeted=False))
    pl.semaphore_wait(barrier, n - 1)
    each(0, GREET, to_owners)
    each(GREET, min(last, steps - 1), lambda i: step(i, True))
    each(last, steps - 1, lambda i: step(i, False))
    step(steps - 1, last == steps, ahead=False)

    @pl.when(owner)
    def _():
        wait(owned.at[pl.ds(0, n - 1)], owned_got)
        wait(owned_stats.at[pl.ds(0, n - 1)], owned_stats_got)
        owned[me] = mine[my_seq]
        owned_stats[me] = mine_stats[my_seq]
        done[my_seq] = merge(owned_stats, [owned])[0]
        others(lambda peer: send(done.at[my_seq], done.at[my_seq], done_sent, done_got, peer))

    for d in range(steps - last):
        wait(direct.at[d, pl.ds(0, n - 1)], direct_got.at[d])
        wait(direct_stats.at[d, pl.ds(0, n - 1)], direct_stats_got.at[d])
        outs = merge(direct_stats.at[d], [direct.at[d, :, g] for g in range(GROUP)])
        for g in range(GROUP):
            o_ref[owners + d * GROUP + g] = outs[g]

    def finish(count):
        wait(done.at[pl.ds(0, owners - count)], done_got)
        wait(mine.at[pl.ds(0, owners - count)], mine_sent)
        wait(mine_stats.at[pl.ds(0, owners - count)], mine_stats_sent)
        if count:
            wait(owned.at[pl.ds(0, n - 1)], done_sent)

    @pl.when(owner)
    def _():
        finish(1)

    if owners < n:

        @pl.when(jnp.logical_not(owner))
        def _():
            finish(0)

    o_ref[pl.ds(0, owners)] = done[...]
    if last < steps:
        wait(direct.at[:, pl.ds(0, n - 1)], direct_sent)
        wait(direct_stats.at[:, pl.ds(0, n - 1)], direct_stats_sent)


def solution(mesh):
    n = mesh.shape["sp"]

    def step(q, k, v):
        batch, tokens, heads, head = k.shape
        owners, late = batch - DIRECT * GROUP, max(DIRECT, 1)
        k, v = (a.reshape(batch, tokens * heads, head) for a in (k, v))
        dma = pltpu.SemaphoreType.DMA
        return pl.pallas_call(
            kernel,
            out_shape=jax.ShapeDtypeStruct(q.shape, q.dtype),
            in_specs=[pl.BlockSpec(memory_space=pltpu.HBM)] * 3,
            out_specs=pl.BlockSpec(memory_space=pltpu.VMEM),
            scratch_shapes=[
                pltpu.VMEM(q.shape, q.dtype),
                pltpu.VMEM((SLOTS, GROUP, tokens * heads, head), k.dtype),
                pltpu.VMEM((SLOTS, GROUP, tokens * heads, head), v.dtype),
                pltpu.VMEM((2, GROUP, heads, tokens * heads), jnp.float32),
                pltpu.VMEM((owners, heads, head), jnp.bfloat16),
                pltpu.VMEM((owners, 2, 128), jnp.float32),
                pltpu.VMEM((n, heads, head), jnp.bfloat16),
                pltpu.VMEM((n, 2, 128), jnp.float32),
                pltpu.VMEM((late, n, GROUP, heads, head), jnp.bfloat16),
                pltpu.VMEM((late, n, 2, 128), jnp.float32),
                pltpu.VMEM((owners, heads, head), jnp.bfloat16),
                dma, dma((SLOTS,)), dma((SLOTS,)), dma, dma, dma, dma, dma, dma, dma, dma, dma((late,)), dma((late,)),
            ],
            compiler_params=pltpu.CompilerParams(collective_id=0, has_side_effects=True, vmem_limit_bytes=40 * 2**20),
        )(pltpu.with_memory_space_constraint(q, pltpu.HBM), k, v)

    return jax.shard_map(
        step,
        mesh=mesh,
        in_specs=(P("dp", None, None), P("dp", "sp", None, None), P("dp", "sp", None, None)),
        out_specs=P("dp", None, None),
        check_vma=False,
    )
```

time: 138 us -> 35.5 us (0.26)
  waiting for transfers between devices: 61.8 us -> 0 us
  matrix products: 37.2 us -> 0 us
  Pallas kernels: 0 us -> 34.8 us
  other arithmetic: 16.8 us -> 0 us
  between operations: 13.5 us -> 0.01 us
  local copies, waits for them, and re-layouts: 8.21 us -> 0.66 us
    all_gather x1 -> x0, waiting for transfers between devices: 61.8 us -> none  [step(): return together(lax.all_gather(part_of(q, k, v), 'sp')).reshape(q.shape)]
    dot_general x2 -> x0, matrix products: 37.2 us -> none  [einsum(): return jnp.einsum(form, a.astype(jnp.float32), b.astype(jnp.float32))]
    pallas_call x0 -> x1, Pallas kernels: none -> 34.8 us  [step(): pl.pallas_call(kernel, out_shape=jax.ShapeDtypeStruct(q.shape, q.dtype),...]
    reduce_sum x2 -> x0, other arithmetic: 11.4 us -> none  [the longest x1 7.13 us: together(): jnp.sum(total * scale, 0)]
    mul x1 -> x0, local copies, waits for them, and re-layouts: 7.67 us -> none  [together(): seen * scale]
    reduce_max x2 -> x0, other arithmetic: 3.64 us -> none  [the longest x1 3.52 us: together(): scale = jnp.exp(high - jnp.max(high, 0))]
  transfers between devices with their start and end apart: 1 -> 0, of which waited for: 1 -> 0; matrix products, arithmetic and copies ran while one was open for 0% -> 0% of each run, Pallas kernels for 0% -> 0%
where the time goes in v2:
time: 35.5 us; the launch traced here: 35.4 us
  Pallas kernels  34.8 us (98%)
  local copies, waits for them, and re-layouts  0.66 us (2%)
    pallas_call x1, Pallas kernels, step(): pl.pallas_call(kernel, out_shape=jax.ShapeDtypeStruct(q.shape, q.dtype),...  34.8 us

profile of v2, /device:TPU:97, one launch (start us, length us, event | category | flops | bytes accessed | tf_op | source)
XLA Modules:
  0.0 35.4 jit_solution(18358984615243392174)
XLA Ops:
  0.0 34.8 %shard_map.37 = bf16[32,8,256]{2,1,0:T(8,128)(2,1)S(1)} custom-call(bf16[32,8,256]{2,1,0:T(8,128)(2,1)} %q_hbm.1, bf16[32,2048,256]{2,1,0:T(8,128)(2,1)} %bitcast.2, bf16[32,2048,256]{2,1,0:T(8,128)(2,1)} %bitcast.3), custom_call_target="tpu_custom_call" | custom-call | tf_op jit(solution)/shard_map/pallas_call | solution.py:193
  34.8 0.7 %copy.5 = bf16[32,8,256]{2,1,0:T(8,128)(2,1)} copy(bf16[32,8,256]{2,1,0:T(8,128)(2,1)S(1)} %shard_map.37) | data formatting | bytes 262144

commit v3 on v2

v3 whole, which is shorter than its diff:
```python
import jax
import jax.numpy as jnp
from jax import lax
from jax.experimental import pallas as pl
from jax.experimental.pallas import tpu as pltpu
from jax.sharding import PartitionSpec as P

MESH = pl.DeviceIdType.MESH
GROUP = 2
SLOTS = 8
GREET = 6


def kernel(
    q_hbm, k_hbm, v_hbm, o_ref, q_ref, kbuf, vbuf, scores, mine, mine_stats, owned, owned_stats, direct, direct_stats, done,
    qsem, ksem, vsem, mine_sent, mine_stats_sent, owned_got, owned_stats_got, done_sent, done_got, direct_sent, direct_stats_sent, direct_got, direct_stats_got,
):
    batch, tokens, head = k_hbm.shape
    heads, n = q_ref.shape[1], owned.shape[0]
    steps, owners = batch // GROUP, done.shape[0]
    me, group = lax.axis_index("sp"), lax.axis_index("dp")
    my_step = owners - 1 - me
    owner = my_step >= 0

    def fetch(hbm, buf, sem, i):
        slot = lax.rem(i, SLOTS)
        return pltpu.make_async_copy(hbm.at[pl.ds(i * GROUP, GROUP)], buf.at[slot], sem.at[slot])

    def values(i, g):
        slot = lax.rem(i, SLOTS)
        return pltpu.make_async_copy(v_hbm.at[i * GROUP + g], vbuf.at[slot, g], vsem.at[slot, g])

    def each(low, high, act):
        def body(i, _):
            act(i)
            return 0

        lax.fori_loop(low, high, body, 0)

    def prefetch(i):
        fetch(k_hbm, kbuf, ksem, i).start()
        for g in range(GROUP):
            values(i, g).start()

    pltpu.make_async_copy(q_hbm, q_ref, qsem).start()
    each(0, min(SLOTS, steps), prefetch)

    def others(act):
        each(0, n - 1, lambda j: act(j + (j >= me).astype(jnp.int32)))

    barrier = pltpu.get_barrier_semaphore()
    others(lambda peer: pl.semaphore_signal(barrier, inc=1, device_id=(group, peer), device_id_type=MESH))

    own = lax.rem(lax.broadcasted_iota(jnp.int32, (heads, tokens), 1), heads) == lax.broadcasted_iota(jnp.int32, (heads, tokens), 0)
    place = lax.broadcasted_iota(jnp.int32, (heads, 128), 1) - lax.broadcasted_iota(jnp.int32, (heads, 128), 0)
    eyes = [place == g * heads for g in range(GROUP)]

    def across(column, g=0):
        return jnp.sum(jnp.where(eyes[g], column, 0.0), 0, keepdims=True)

    def down(line, g=0):
        return jnp.sum(jnp.where(eyes[g], line, 0.0), 1, keepdims=True)

    def send(src, dst, sent, got, peer):
        pltpu.make_async_remote_copy(src_ref=src, dst_ref=dst, send_sem=sent, recv_sem=got, device_id=(group, peer), device_id_type=MESH).start()

    def wait(ref, sem):
        pltpu.make_async_copy(ref, ref, sem).wait()

    def score(i):
        slot = lax.rem(i, SLOTS)
        for g in range(GROUP):
            scores[lax.rem(i, 2), g] = lax.dot_general(q_ref[i * GROUP + g], kbuf[slot, g], (((1,), (1,)), ((), ())), preferred_element_type=jnp.float32)

    def attend(i, final):
        slot = lax.rem(i, SLOTS)
        weights, highs, totals = [], [], []
        for g in range(GROUP):
            s = jnp.where(own, scores[lax.rem(i, 2), g] * head**-0.5, -jnp.inf)
            high = jnp.max(s, 1, keepdims=True)
            w = jnp.exp(s - high)
            weights.append(w.astype(jnp.bfloat16))
            highs.append(across(high, g))
            totals.append(across(jnp.sum(w, 1, keepdims=True), g))
        stats = jnp.concatenate([sum(highs), sum(totals)], 0)
        if final:
            direct_stats[me] = stats
        else:
            mine_stats[i] = stats
        for g in range(GROUP):
            if final:
                values(i, g).wait()
            seen = jnp.dot(weights[g], vbuf[slot, g], preferred_element_type=jnp.float32).astype(jnp.bfloat16)
            if final:
                direct[me, g] = seen
            else:
                mine[i, g] = seen

    def to_all():
        def both(peer):
            send(direct.at[me], direct.at[me], direct_sent, direct_got, peer)
            send(direct_stats.at[me], direct_stats.at[me], direct_stats_sent, direct_stats_got, peer)

        others(both)

    def to_owner(i):
        to = owners - 1 - i

        @pl.when(me != to)
        def _():
            send(mine.at[i], owned.at[me], mine_sent, owned_got, to)
            send(mine_stats.at[i], owned_stats.at[me], mine_stats_sent, owned_stats_got, to)

    def merge(stats, parts):
        high = stats[:, 0, :]
        top = jnp.max(high, 0, keepdims=True)
        scale = jnp.exp(high - top)
        total = jnp.sum(stats[:, 1, :] * scale, 0, keepdims=True)
        outs = []
        for g in range(GROUP):
            seen = sum(down(scale[s : s + 1], g) * parts[s, g].astype(jnp.float32) for s in range(n))
            outs.append((seen / down(total, g)).astype(jnp.bfloat16))
        return jnp.stack(outs)

    def step(i, greeted):
        fetch(k_hbm, kbuf, ksem, i + 1).wait()
        for g in range(GROUP):
            values(i, g).wait()
        score(i + 1)
        attend(i, False)
        if greeted:
            to_owner(i)

        @pl.when(i + SLOTS < steps)
        def _():
            prefetch(i + SLOTS)

    wait(q_ref, qsem)
    fetch(k_hbm, kbuf, ksem, 0).wait()
    score(0)
    each(0, GREET, lambda i: step(i, False))
    pl.semaphore_wait(barrier, n - 1)
    each(0, GREET, to_owner)
    each(GREET, steps - 1, lambda i: step(i, True))
    attend(steps - 1, True)
    to_all()

    @pl.when(owner)
    def _():
        wait(owned.at[pl.ds(0, n - 1)], owned_got)
        wait(owned_stats.at[pl.ds(0, n - 1)], owned_stats_got)
        owned[me] = mine[my_step]
        owned_stats[me] = mine_stats[my_step]
        done[my_step] = merge(owned_stats, owned)
        others(lambda peer: send(done.at[my_step], done.at[my_step], done_sent, done_got, peer))

    wait(direct.at[pl.ds(0, n - 1)], direct_got)
    wait(direct_stats.at[pl.ds(0, n - 1)], direct_stats_got)
    o_ref[pl.ds(owners * GROUP, GROUP)] = merge(direct_stats, direct)

    def finish(count):
        wait(done.at[pl.ds(0, owners - count)], done_got)
        wait(mine.at[pl.ds(0, owners - count)], mine_sent)
        wait(mine_stats.at[pl.ds(0, owners - count)], mine_stats_sent)
        if count:
            wait(owned.at[pl.ds(0, n - 1)], done_sent)

    @pl.when(owner)
    def _():
        finish(1)

    @pl.when(jnp.logical_not(owner))
    def _():
        finish(0)

    o_ref[pl.ds(0, owners * GROUP)] = done[...].reshape(owners * GROUP, heads, head)
    wait(direct.at[pl.ds(0, n - 1)], direct_sent)
    wait(direct_stats.at[pl.ds(0, n - 1)], direct_stats_sent)


def solution(mesh):
    n = mesh.shape["sp"]

    def step(q, k, v):
        batch, tokens, heads, head = k.shape
        owners = batch // GROUP - 1
        k, v = (a.reshape(batch, tokens * heads, head) for a in (k, v))
        dma = pltpu.SemaphoreType.DMA
        return pl.pallas_call(
            kernel,
            out_shape=jax.ShapeDtypeStruct(q.shape, q.dtype),
            in_specs=[pl.BlockSpec(memory_space=pltpu.HBM)] * 3,
            out_specs=pl.BlockSpec(memory_space=pltpu.VMEM),
            scratch_shapes=[
                pltpu.VMEM(q.shape, q.dtype),
                pltpu.VMEM((SLOTS, GROUP, tokens * heads, head), k.dtype),
                pltpu.VMEM((SLOTS, GROUP, tokens * heads, head), v.dtype),
                pltpu.VMEM((2, GROUP, heads, tokens * heads), jnp.float32),
                pltpu.VMEM((owners, GROUP, heads, head), jnp.bfloat16),
                pltpu.VMEM((owners, 2, 128), jnp.float32),
                pltpu.VMEM((n, GROUP, heads, head), jnp.bfloat16),
                pltpu.VMEM((n, 2, 128), jnp.float32),
                pltpu.VMEM((n, GROUP, heads, head), jnp.bfloat16),
                pltpu.VMEM((n, 2, 128), jnp.float32),
                pltpu.VMEM((owners, GROUP, heads, head), jnp.bfloat16),
                dma, dma((SLOTS,)), dma((SLOTS, GROUP)), dma, dma, dma, dma, dma, dma, dma, dma, dma, dma,
            ],
            compiler_params=pltpu.CompilerParams(collective_id=0, has_side_effects=True, vmem_limit_bytes=40 * 2**20),
        )(pltpu.with_memory_space_constraint(q, pltpu.HBM), k, v)

    return jax.shard_map(
        step,
        mesh=mesh,
        in_specs=(P("dp", None, None), P("dp", "sp", None, None), P("dp", "sp", None, None)),
        out_specs=P("dp", None, None),
        check_vma=False,
    )
```

time: 35.5 us -> 34.6 us (0.975)
  Pallas kernels: 34.8 us -> 33.9 us
    pallas_call x1, Pallas kernels: 34.8 us -> 33.9 us  [step(): pl.pallas_call(kernel, out_shape=jax.ShapeDtypeStruct(q.shape, q.dtype),...]
where the time goes in v3:
time: 34.6 us; the launch traced here: 34.5 us
  Pallas kernels  33.9 us (98%)
  local copies, waits for them, and re-layouts  0.66 us (2%)
    pallas_call x1, Pallas kernels, step(): pl.pallas_call(kernel, out_shape=jax.ShapeDtypeStruct(q.shape, q.dtype),...  33.9 us

profile of v3, /device:TPU:97, one launch (start us, length us, event | category | flops | bytes accessed | tf_op | source)
XLA Modules:
  0.0 34.5 jit_solution(15054857865923992651)
XLA Ops:
  0.0 33.9 %shard_map.37 = bf16[32,8,256]{2,1,0:T(8,128)(2,1)S(1)} custom-call(bf16[32,8,256]{2,1,0:T(8,128)(2,1)} %q_hbm.1, bf16[32,2048,256]{2,1,0:T(8,128)(2,1)} %bitcast.2, bf16[32,2048,256]{2,1,0:T(8,128)(2,1)} %bitcast.3), custom_call_target="tpu_custom_call" | custom-call | tf_op jit(solution)/shard_map/pallas_call | solution.py:189
  33.9 0.7 %copy.5 = bf16[32,8,256]{2,1,0:T(8,128)(2,1)} copy(bf16[32,8,256]{2,1,0:T(8,128)(2,1)S(1)} %shard_map.37) | data formatting | bytes 262144

commit v4 on v3

v4 whole, which is shorter than its diff:
```python
import math

import jax
import jax.numpy as jnp
from jax import lax
from jax.experimental import pallas as pl
from jax.experimental.pallas import tpu as pltpu
from jax.sharding import PartitionSpec as P

MESH = pl.DeviceIdType.MESH
CORES = 2
GROUP = 2
SLOTS = 4
GREET = 6


def kernel(
    q_hbm, k_hbm, v_hbm, o_ref, q_ref, kbuf, vbuf, scores, mine, mine_stats, owned, owned_stats, done,
    qsem, ksem, vsem, mine_sent, mine_stats_sent, owned_got, owned_stats_got, done_sent, done_got,
):
    batch, tokens, head = k_hbm.shape
    heads, n = q_ref.shape[1], owned.shape[0]
    steps, owners = batch // GROUP, done.shape[0]
    outer = math.isqrt(n // CORES)
    inner = n // outer
    me, group = lax.axis_index("sp"), lax.axis_index("dp")
    my_step = owners - 1 - me
    owner = my_step >= 0

    def fetch(hbm, buf, sem, i):
        slot = lax.rem(i, SLOTS)
        return pltpu.make_async_copy(hbm.at[pl.ds(i * GROUP, GROUP)], buf.at[slot], sem.at[slot])

    def each(low, high, act):
        def body(i, _):
            act(i)
            return 0

        lax.fori_loop(low, high, body, 0)

    def prefetch(i):
        @pl.when(i + 1 < steps)
        def _():
            fetch(k_hbm, kbuf, ksem, i + 1).start()

        @pl.when(i < steps)
        def _():
            fetch(v_hbm, vbuf, vsem, i).start()

    pltpu.make_async_copy(q_hbm, q_ref, qsem).start()
    fetch(k_hbm, kbuf, ksem, 0).start()
    each(0, SLOTS - 1, prefetch)

    def others(act):
        each(0, n - 1, lambda j: act(j + (j >= me).astype(jnp.int32)))

    barrier = pltpu.get_barrier_semaphore()
    others(lambda peer: pl.semaphore_signal(barrier, inc=1, device_id=(group, peer), device_id_type=MESH))

    own = lax.rem(lax.broadcasted_iota(jnp.int32, (heads, tokens), 1), heads) == lax.broadcasted_iota(jnp.int32, (heads, tokens), 0)
    place = lax.broadcasted_iota(jnp.int32, (heads, 128), 1) - lax.broadcasted_iota(jnp.int32, (heads, 128), 0)
    eyes = [place == g * heads for g in range(GROUP)]

    def across(column, g=0):
        return jnp.sum(jnp.where(eyes[g], column, 0.0), 0, keepdims=True)

    def down(line, g=0):
        return jnp.sum(jnp.where(eyes[g], line, 0.0), 1, keepdims=True)

    def send(src, dst, sent, got, peer):
        pltpu.make_async_remote_copy(src_ref=src, dst_ref=dst, send_sem=sent, recv_sem=got, device_id=(group, peer), device_id_type=MESH).start()

    def wait(ref, sem):
        pltpu.make_async_copy(ref, ref, sem).wait()

    def score(i):
        slot = lax.rem(i, SLOTS)
        for g in range(GROUP):
            scores[lax.rem(i, 2), g] = lax.dot_general(q_ref[i * GROUP + g], kbuf[slot, g], (((1,), (1,)), ((), ())), preferred_element_type=jnp.float32)

    def weigh(i):
        weights, highs, totals = [], [], []
        for g in range(GROUP):
            s = jnp.where(own, scores[lax.rem(i, 2), g] * head**-0.5, -jnp.inf)
            high = jnp.max(s, 1, keepdims=True)
            w = jnp.exp(s - high)
            weights.append(w.astype(jnp.bfloat16))
            highs.append(across(high, g))
            totals.append(across(jnp.sum(w, 1, keepdims=True), g))
        return weights, jnp.concatenate([sum(highs), sum(totals)], 0)

    def see(i, weights, part):
        slot = lax.rem(i, SLOTS)
        for g in range(GROUP):
            part[g] = jnp.dot(weights[g], vbuf[slot, g], preferred_element_type=jnp.float32).astype(jnp.bfloat16)

    def attend(i):
        weights, mine_stats[i] = weigh(i)
        see(i, weights, mine.at[i])

    def to_owner(i):
        to = owners - 1 - i

        @pl.when(me != to)
        def _():
            send(mine.at[i], owned.at[me], mine_sent, owned_got, to)
            send(mine_stats.at[i], owned_stats.at[me], mine_stats_sent, owned_stats_got, to)

    def merge(stats, parts):
        high = stats[:, 0, :]
        top = jnp.max(high, 0, keepdims=True)
        scale = jnp.exp(high - top)
        total = jnp.sum(stats[:, 1, :] * scale, 0, keepdims=True)
        outs = []
        for g in range(GROUP):
            seen = sum(down(scale[s : s + 1], g) * parts[s, g].astype(jnp.float32) for s in range(n))
            outs.append((seen / down(total, g)).astype(jnp.bfloat16))
        return jnp.stack(outs)

    def step(i):
        @pl.when(i == GREET)
        def _():
            pl.semaphore_wait(barrier, n - 1)
            each(0, GREET, to_owner)

        fetch(k_hbm, kbuf, ksem, i + 1).wait()
        fetch(v_hbm, vbuf, vsem, i).wait()
        attend(i)
        score(i + 1)
        pl.when(i >= GREET)(lambda: to_owner(i))
        prefetch(i + SLOTS)

    wait(q_ref, qsem)
    fetch(k_hbm, kbuf, ksem, 0).wait()
    score(0)
    prefetch(SLOTS - 1)
    each(0, steps - 2, step)
    fetch(k_hbm, kbuf, ksem, steps - 1).wait()
    score(steps - 1)
    fetch(v_hbm, vbuf, vsem, steps - 2).wait()
    attend(steps - 2)
    weights, mine_stats[steps - 1] = weigh(steps - 1)
    to_owner(steps - 2)
    fetch(v_hbm, vbuf, vsem, steps - 1).wait()
    see(steps - 1, weights, mine.at[steps - 1])
    to_owner(steps - 1)

    @pl.when(owner)
    def _():
        wait(owned.at[pl.ds(0, n - 1)], owned_got)
        wait(owned_stats.at[pl.ds(0, n - 1)], owned_stats_got)
        owned[me] = mine[my_step]
        owned_stats[me] = mine_stats[my_step]
        done[my_step] = merge(owned_stats, owned)
        row, rest = lax.div(me, inner), lax.rem(me, inner)
        turn = (lax.div(rest, CORES) * outer + row) * CORES + lax.rem(rest, CORES)

        def tell(j):
            k = j + (j >= turn).astype(jnp.int32)
            peer = lax.rem(lax.div(k, CORES), outer) * inner + lax.div(k, CORES * outer) * CORES + lax.rem(k, CORES)
            send(done.at[my_step], done.at[my_step], done_sent, done_got, peer)

        each(0, n - 1, tell)

    def finish(count):
        wait(done.at[pl.ds(0, owners - count)], done_got)
        wait(mine.at[pl.ds(0, owners - count)], mine_sent)
        wait(mine_stats.at[pl.ds(0, owners - count)], mine_stats_sent)
        if count:
            wait(owned.at[pl.ds(0, n - 1)], done_sent)

    @pl.when(owner)
    def _():
        finish(1)

    @pl.when(jnp.logical_not(owner))
    def _():
        finish(0)

    o_ref[...] = done[...].reshape(batch, heads, head)


def solution(mesh):
    n = mesh.shape["sp"]

    def step(q, k, v):
        batch, tokens, heads, head = k.shape
        owners = batch // GROUP
        k, v = (a.reshape(batch, tokens * heads, head) for a in (k, v))
        dma = pltpu.SemaphoreType.DMA
        return pl.pallas_call(
            kernel,
            out_shape=jax.ShapeDtypeStruct(q.shape, q.dtype),
            in_specs=[pl.BlockSpec(memory_space=pltpu.HBM)] * 3,
            out_specs=pl.BlockSpec(memory_space=pltpu.VMEM),
            scratch_shapes=[
                pltpu.VMEM(q.shape, q.dtype),
                pltpu.VMEM((SLOTS, GROUP, tokens * heads, head), k.dtype),
                pltpu.VMEM((SLOTS, GROUP, tokens * heads, head), v.dtype),
                pltpu.VMEM((2, GROUP, heads, tokens * heads), jnp.float32),
                pltpu.VMEM((owners, GROUP, heads, head), jnp.bfloat16),
                pltpu.VMEM((owners, 2, 128), jnp.float32),
                pltpu.VMEM((n, GROUP, heads, head), jnp.bfloat16),
                pltpu.VMEM((n, 2, 128), jnp.float32),
                pltpu.VMEM((owners, GROUP, heads, head), jnp.bfloat16),
                dma, dma((SLOTS,)), dma((SLOTS,)), dma, dma, dma, dma, dma, dma,
            ],
            compiler_params=pltpu.CompilerParams(collective_id=0, has_side_effects=True, vmem_limit_bytes=24 * 2**20),
        )(pltpu.with_memory_space_constraint(q, pltpu.HBM), k, v)

    return jax.shard_map(
        step,
        mesh=mesh,
        in_specs=(P("dp", None, None), P("dp", "sp", None, None), P("dp", "sp", None, None)),
        out_specs=P("dp", None, None),
        check_vma=False,
    )
```

time: 34.6 us -> 34.3 us (level)
  no operation moved by 1% of the time
where the time goes in v4:
time: 34.3 us; the launch traced here: 34.2 us
  Pallas kernels  33.6 us (98%)
  local copies, waits for them, and re-layouts  0.66 us (2%)
    pallas_call x1, Pallas kernels, step(): pl.pallas_call(kernel, out_shape=jax.ShapeDtypeStruct(q.shape, q.dtype),...  33.6 us

profile of v4, /device:TPU:97, one launch (start us, length us, event | category | flops | bytes accessed | tf_op | source)
XLA Modules:
  0.0 34.2 jit_solution(1585244420093973511)
XLA Ops:
  0.0 33.6 %shard_map.37 = bf16[32,8,256]{2,1,0:T(8,128)(2,1)S(1)} custom-call(bf16[32,8,256]{2,1,0:T(8,128)(2,1)} %q_hbm.1, bf16[32,2048,256]{2,1,0:T(8,128)(2,1)} %bitcast.2, bf16[32,2048,256]{2,1,0:T(8,128)(2,1)} %bitcast.3), custom_call_target="tpu_custom_call" | custom-call | tf_op jit(solution)/shard_map/pallas_call | solution.py:191
  33.6 0.7 %copy.5 = bf16[32,8,256]{2,1,0:T(8,128)(2,1)} copy(bf16[32,8,256]{2,1,0:T(8,128)(2,1)S(1)} %shard_map.37) | data formatting | bytes 262144

commit v5 on v4

--- a/solution.py
+++ b/solution.py
@@ -10,7 +10,7 @@
 MESH = pl.DeviceIdType.MESH
 CORES = 2
 GROUP = 2
-SLOTS = 4
+SLOTS = 3
 GREET = 6
 
 
@@ -154,13 +154,10 @@
         done[my_step] = merge(owned_stats, owned)
         row, rest = lax.div(me, inner), lax.rem(me, inner)
         turn = (lax.div(rest, CORES) * outer + row) * CORES + lax.rem(rest, CORES)
-
-        def tell(j):
+        for j in range(n - 1):
             k = j + (j >= turn).astype(jnp.int32)
             peer = lax.rem(lax.div(k, CORES), outer) * inner + lax.div(k, CORES * outer) * CORES + lax.rem(k, CORES)
             send(done.at[my_step], done.at[my_step], done_sent, done_got, peer)
-
-        each(0, n - 1, tell)
 
     def finish(count):
         wait(done.at[pl.ds(0, owners - count)], done_got)

time: 34.3 us -> 34.3 us (level)
  no operation moved by 1% of the time
where the time goes in v5:
time: 34.3 us; the launch traced here: 34.2 us
  Pallas kernels  33.5 us (98%)
  local copies, waits for them, and re-layouts  0.66 us (2%)
    pallas_call x1, Pallas kernels, step(): pl.pallas_call(kernel, out_shape=jax.ShapeDtypeStruct(q.shape, q.dtype),...  33.5 us

profile of v5, /device:TPU:97, one launch (start us, length us, event | category | flops | bytes accessed | tf_op | source)
XLA Modules:
  0.0 34.2 jit_solution(6477120738498510931)
XLA Ops:
  0.0 33.5 %shard_map.37 = bf16[32,8,256]{2,1,0:T(8,128)(2,1)S(1)} custom-call(bf16[32,8,256]{2,1,0:T(8,128)(2,1)} %q_hbm.1, bf16[32,2048,256]{2,1,0:T(8,128)(2,1)} %bitcast.2, bf16[32,2048,256]{2,1,0:T(8,128)(2,1)} %bitcast.3), custom_call_target="tpu_custom_call" | custom-call | tf_op jit(solution)/shard_map/pallas_call | solution.py:188
  33.5 0.7 %copy.5 = bf16[32,8,256]{2,1,0:T(8,128)(2,1)} copy(bf16[32,8,256]{2,1,0:T(8,128)(2,1)S(1)} %shard_map.37) | data formatting | bytes 262144
